TPU v7x, 32 devices: a whole 2x2x4 slice. The times are simulated.
32 devices in a mesh: cfg: 2 (over core), tm: 16 (over z, y, x).
Axes of the slice: x: 2, y: 2, z: 4, core: 2. Of those that a mesh axis runs over, the one named last changes fastest.
Arguments:
- queries: bfloat16 [2, 12288, 1152], P('cfg', 'tm'), may hold values from -6 to 6
- key_vectors: bfloat16 [2, 12288, 1152], P('cfg', 'tm'), may hold values from -12 to 12
- value_vectors: bfloat16 [2, 12288, 1152], P('cfg', 'tm'), may hold values from -4 to 4
- out_weight: bfloat16 [1152, 2240], replicated, may hold values from -0.1875 to 0.1875
- first_frame: int32 [32], P('tm'), may hold values from 0 to 31, as said below
Outputs:
- guided: bfloat16 [12288, 2240], P('tm', 'cfg')
Inputs may be any that keep to these rules, and one draw needn't show every extreme that they name: first_frame[f] is 0 or lies between f - 4 and f; some frame f has first_frame[f] = f - 4.
All inputs are finite; a program needn't handle non-finite values.
Results may differ from a plain program's by a relative error of at most 0.014.
Values may be sent and summed in bfloat16 or wider, within the bound.
A program may use at most 192 MiB of HBM per device.

v0:
```python
import functools

import jax
import jax.numpy as jnp
from jax import lax
from jax.experimental import pallas as pl
from jax.experimental.pallas import tpu as pltpu
from jax.sharding import PartitionSpec as P

DH = 32
NEAR = 2
LANES = 128
PER = LANES // DH
CHUNKS = 3

guide_scale = 4.5
epsilon = 1e-06


def head_mask(rows, block):
    row = lax.broadcasted_iota(jnp.int32, (rows, LANES), 0) // DH
    lane = lax.broadcasted_iota(jnp.int32, (rows, LANES), 1) // DH
    return lane == (block if rows == DH else row)


def split_rows(height):
    units = height // 16
    sizes = [(units * (c + 1)) // CHUNKS - (units * c) // CHUNKS for c in range(CHUNKS)]
    return [(16 * sum(sizes[:c]), 16 * sizes[c]) for c in range(CHUNKS)]


def guided_kernel(
    n, bits, ff_ref, q_ref, k_ref, v_ref, w_ref, o_ref,
    kbuf, vbuf, qbuf, wbuf, own_att, comb, obuf, frames, near_out, near_in, tot, pre, tot_out, tot_in, fin, other,
    load_sem, late_sem, out_sem, tot_send, tot_recv, near_send, near_recv, q_sem, fin_sem,
):
    fr = frames.shape[0]
    ft = kbuf.shape[0] // fr
    groups = kbuf.shape[1] // LANES
    base = groups * DH
    chunks = split_rows(frames.shape[1])
    me = lax.axis_index("tm")
    other_core = 1 - lax.axis_index("cfg")

    loads = []
    for f in range(fr):
        rows = pl.ds(f * ft, ft)
        for which, (src, dst) in enumerate(((k_ref, kbuf), (v_ref, vbuf))):
            copy = pltpu.make_async_copy(src.at[rows], dst.at[rows], load_sem.at[2 * f + which])
            copy.start()
            loads.append(copy)

    def partner(k):
        bit = (me // (1 << k)) % 2
        return bit, me + (1 - 2 * bit) * (1 << k)

    barrier = pltpu.get_barrier_semaphore()
    pl.semaphore_signal(barrier, inc=1, device_id={"cfg": other_core})
    count = jnp.int32(1 + bits)
    for k in range(bits):
        pl.semaphore_signal(barrier, inc=1, device_id={"tm": partner(k)[1]})
    for d in range(1, NEAR + 1):
        @pl.when(me + d < n)
        def _():
            pl.semaphore_signal(barrier, inc=1, device_id={"tm": me + d})

        @pl.when(me >= d)
        def _():
            pl.semaphore_signal(barrier, inc=1, device_id={"tm": me - d})

        count = count + jnp.where(me + d < n, 1, 0) + jnp.where(me >= d, 1, 0)

    masks = [head_mask(DH, a) for a in range(PER)]
    for f in range(fr):
        loads[2 * f].wait()
        loads[2 * f + 1].wait()
        frames[f, base:, :] = jnp.zeros((frames.shape[1] - base, LANES), jnp.float32)
        for g in range(groups):
            cols = slice(g * LANES, (g + 1) * LANES)
            keys = jnp.maximum(kbuf[f * ft:(f + 1) * ft, cols], 0)
            values = vbuf[f * ft:(f + 1) * ft, cols]
            full = lax.dot_general(
                values, keys, (((0,), (0,)), ((), ())), preferred_element_type=jnp.float32
            )
            compact = jnp.zeros((DH, LANES), jnp.float32)
            for a in range(PER):
                compact = jnp.where(masks[a], full[a * DH:(a + 1) * DH], compact)
            frames[f, g * DH:(g + 1) * DH, :] = compact
            frames[f, base + g:base + g + 1, :] = jnp.sum(
                keys.astype(jnp.float32), axis=0, keepdims=True
            )
    columns = wbuf.shape[0]
    late = [
        pltpu.make_async_copy(q_ref, qbuf.at[0], late_sem.at[0]),
        pltpu.make_async_copy(
            w_ref.at[pl.ds(pl.multiple_of((1 - other_core) * columns, 16), columns)],
            wbuf, late_sem.at[1],
        ),
    ]
    for copy in late:
        copy.start()
    near_out[...] = frames[...].astype(jnp.bfloat16)
    total = frames[0]
    for f in range(1, fr):
        total = total + frames[f]
    tot[...] = total
    tot_out[0] = total.astype(jnp.bfloat16)
    pre[...] = jnp.zeros_like(pre)
    for d in range(1, NEAR + 1):
        @pl.when(me < d)
        def _():
            near_in[d - 1] = jnp.zeros(near_in.shape[1:], jnp.bfloat16)

    pl.semaphore_wait(barrier, count)

    def near_copy(d):
        return pltpu.make_async_remote_copy(
            src_ref=near_out, dst_ref=near_in.at[d - 1], send_sem=near_send.at[d - 1],
            recv_sem=near_recv.at[d - 1], device_id={"tm": me + d},
        )

    def start_near(d):
        @pl.when(me + d < n)
        def _():
            near_copy(d).start()

    q_copy = pltpu.make_async_remote_copy(
        src_ref=q_ref, dst_ref=qbuf.at[1], send_sem=q_sem.at[0], recv_sem=q_sem.at[1],
        device_id={"cfg": other_core},
    )
    def total_copy(k, c):
        part = pl.ds(*chunks[c])
        return pltpu.make_async_remote_copy(
            src_ref=tot_out.at[k, part], dst_ref=tot_in.at[k, part],
            send_sem=tot_send.at[k, c], recv_sem=tot_recv.at[k, c],
            device_id={"tm": partner(k)[1]},
        )

    def send_total(k, c):
        if k < bits - 1:
            total_copy(k, c).start()
        else:
            @pl.when(partner(k)[0] == 0)
            def _():
                total_copy(k, c).start()

    for c in range(len(chunks)):
        send_total(0, c)
    start_near(2)
    q_copy.start()
    for k in range(bits):
        bit = partner(k)[0]
        for c, (lo, size) in enumerate(chunks):
            part = slice(lo, lo + size)
            if k < bits - 1:
                total_copy(k, c).wait_recv()
                got = tot_in[k, part].astype(jnp.float32)
                pre[part] += jnp.where(bit == 1, 1.0, 0.0) * got
                summed = tot[part] + got
                tot[part] = summed
                tot_out[k + 1, part] = summed.astype(jnp.bfloat16)
                send_total(k + 1, c)
            else:
                @pl.when(bit == 1)
                def _():
                    total_copy(k, c).wait_recv()
                    pre[part] += tot_in[k, part].astype(jnp.float32)
        if k == 0:
            start_near(1)
    for k in range(bits):
        for c in range(len(chunks)):
            if k < bits - 1:
                total_copy(k, c).wait_send()
            else:
                @pl.when(partner(k)[0] == 0)
                def _():
                    total_copy(k, c).wait_send()

    for d in range(1, NEAR + 1):
        @pl.when(me >= d)
        def _():
            near_copy(d).wait_recv()

        @pl.when(me + d < n)
        def _():
            near_copy(d).wait_send()

    for j in range(fr):
        first = ff_ref[j]
        whole = first == 0
        acc = jnp.where(whole, 1.0, 0.0) * pre[...]
        for f in range(j + 1):
            acc = acc + jnp.where(me * fr + f >= first, 1.0, 0.0) * frames[f]
        for d in range(1, NEAR + 1):
            for f in range(fr):
                inside = jnp.logical_and(first > 0, (me - d) * fr + f >= first)
                acc = acc + jnp.where(inside, 1.0, 0.0) * near_in[d - 1, f].astype(jnp.float32)
        fin[j] = acc
    fin_copy = pltpu.make_async_remote_copy(
        src_ref=fin, dst_ref=other, send_sem=fin_sem.at[0], recv_sem=fin_sem.at[1],
        device_id={"cfg": other_core},
    )
    fin_copy.start()

    own_scale = jnp.where(other_core == 1, guide_scale, 1.0 - guide_scale)
    other_scale = 1.0 - own_scale
    diagonal = head_mask(LANES, 0)
    tile = ft if ft % 256 == 0 else 2 * LANES

    def attended(b, source, f, g):
        rows = slice(f * ft, (f + 1) * ft)
        cols = slice(g * LANES, (g + 1) * LANES)
        compact = source[f, g * DH:(g + 1) * DH, :]
        sums = source[f, base + g:base + g + 1, :]
        state = jnp.where(diagonal, jnp.concatenate([compact] * PER, axis=0), 0.0)
        total = jnp.where(diagonal, jnp.broadcast_to(sums, (LANES, LANES)), 0.0)
        both = jnp.concatenate([state, total], axis=0)
        upper = both.astype(jnp.bfloat16)
        lower = (both - upper.astype(jnp.float32)).astype(jnp.bfloat16)
        feats = jnp.maximum(qbuf[b, rows, cols], 0)
        both = lax.dot_general(
            jnp.concatenate([feats, feats], axis=1),
            jnp.concatenate([upper, lower], axis=1),
            (((1,), (1,)), ((), ())), preferred_element_type=jnp.float32,
        )
        return rows, cols, both[:, :LANES] / (both[:, LANES:] + epsilon)

    late[0].wait()
    for f in range(fr):
        for g in range(groups):
            rows, cols, value = attended(0, fin, f, g)
            own_att[rows, cols] = own_scale * value
    fin_copy.wait()
    q_copy.wait()
    for f in range(fr):
        for g in range(groups):
            rows, cols, value = attended(1, other, f, g)
            comb[rows, cols] = (own_att[rows, cols] + other_scale * value).astype(jnp.bfloat16)
    late[1].wait()
    outs = []
    for t in range(comb.shape[0] // tile):
        part = slice(t * tile, (t + 1) * tile)
        obuf[:, part] = lax.dot_general(
            wbuf[...], comb[part, :], (((1,), (1,)), ((), ())),
            preferred_element_type=jnp.float32,
        ).astype(obuf.dtype)
        span = pl.ds(t * tile, tile)
        copy = pltpu.make_async_copy(obuf.at[:, span], o_ref.at[:, span], out_sem.at[t])
        copy.start()
        outs.append(copy)
    for copy in outs:
        copy.wait()


def on_device(n, cores, queries, key_vectors, value_vectors, out_weight, first_frame):
    rows, width = queries.shape[1:]
    fr = first_frame.shape[0]
    bits = n.bit_length() - 1
    groups = width // LANES
    height = groups * DH + 16 * pl.cdiv(groups, 16)
    block = (height, LANES)
    flat = lambda a: a.reshape(rows, width)
    queries = flat(queries)
    f32, bf16 = jnp.float32, jnp.bfloat16
    hbm = pl.BlockSpec(memory_space=pltpu.HBM)
    columns = out_weight.shape[1] // cores
    flipped = pl.pallas_call(
        functools.partial(guided_kernel, n, bits),
        name="guided",
        out_shape=jax.ShapeDtypeStruct((columns, rows), bf16),
        in_specs=[pl.BlockSpec(memory_space=pltpu.SMEM), hbm, hbm, hbm, hbm],
        out_specs=hbm,
        scratch_shapes=[
            pltpu.VMEM((rows, width), bf16),
            pltpu.VMEM((rows, width), bf16),
            pltpu.VMEM((2, rows, width), bf16),
            pltpu.VMEM((columns, width), bf16),
            pltpu.VMEM((rows, width), f32),
            pltpu.VMEM((rows, width), bf16),
            pltpu.VMEM((columns, rows), bf16),
            pltpu.VMEM((fr,) + block, f32),
            pltpu.VMEM((fr,) + block, bf16),
            pltpu.VMEM((NEAR, fr) + block, bf16),
            pltpu.VMEM(block, f32),
            pltpu.VMEM(block, f32),
            pltpu.VMEM((bits,) + block, bf16),
            pltpu.VMEM((bits,) + block, bf16),
            pltpu.VMEM((fr,) + block, f32),
            pltpu.VMEM((fr,) + block, f32),
            pltpu.SemaphoreType.DMA((2 * fr,)),
            pltpu.SemaphoreType.DMA((2,)),
            pltpu.SemaphoreType.DMA((rows // LANES,)),
            pltpu.SemaphoreType.DMA((bits, CHUNKS)),
            pltpu.SemaphoreType.DMA((bits, CHUNKS)),
            pltpu.SemaphoreType.DMA((NEAR,)),
            pltpu.SemaphoreType.DMA((NEAR,)),
            pltpu.SemaphoreType.DMA((2,)),
            pltpu.SemaphoreType.DMA((2,)),
        ],
        compiler_params=pltpu.CompilerParams(
            collective_id=0, has_side_effects=True
        ),
    )(first_frame, queries, flat(key_vectors), flat(value_vectors), out_weight.T)

    return flipped.T


def solution(mesh):
    placed = (P("cfg", "tm", None), P("cfg", "tm", None), P("cfg", "tm", None), P(), P("tm"))
    return jax.shard_map(
        functools.partial(on_device, mesh.shape["tm"], mesh.shape["cfg"]),
        mesh=mesh, in_specs=placed, out_specs=P("tm", "cfg"), check_vma=False,
    )
```

profile of v0, /device:TPU:0, one launch (start us, length us, event | category | flops | bytes accessed | tf_op | source)
XLA Modules:
  0.0 29.1 jit_solution(13930676131886402689)
XLA Ops:
  0.0 26.3 %guided.1 = bf16[1120,768]{1,0:T(8,128)(2,1)} custom-call(s32[2]{0:T(128)} %ff_ref.1, bf16[768,1152]{1,0:T(8,128)(2,1)} %bitcast.7, bf16[768,1152]{1,0:T(8,128)(2,1)} %bitcast.8, bf16[768,1152]{1,0:T(8,128)(2,1)} %bitcast.9, bf16[2240,1152]{1,0:T(8,128)(2,1)} %bitcast.6), custom_call_target="tpu_custom_call" | custom-call | tf_op jit(solution)/shard_map/guided/pallas_call | solution.py:267
  26.3 2.8 %copy.7 = bf16[768,1120]{0,1:T(8,128)(2,1)} copy(bf16[768,1120]{0,1:T(8,128)(2,1)} %bitcast.5) | data formatting | bytes 3440640
where the time goes:
time: 29.3 us; the launch traced here: 29.1 us
  Pallas kernels  26.3 us (90%)
  local copies, waits for them, and re-layouts  2.76 us (9%)
    pallas_call x1, Pallas kernels, on_device(): pl.pallas_call(functools.partial(guided_kernel, n, bits), name='guided',...  26.3 us
    unnamed x1, local copies, waits for them, and re-layouts  2.76 us

commit v1 on v0

v1 whole, which is shorter than its diff:
```python
import functools

import jax
import jax.numpy as jnp
from jax import lax
from jax.experimental import pallas as pl
from jax.experimental.pallas import tpu as pltpu
from jax.sharding import PartitionSpec as P

DH = 32
NEAR = 2
LANES = 128
PER = LANES // DH
GROUP = 4
TILE = 256
PARTS = 2
SPLIT = (4, 3, 2)
VMEM_BYTES = 67043328

guide_scale = 4.5
epsilon = 1e-06


def head_mask(rows, block):
    row = lax.broadcasted_iota(jnp.int32, (rows, LANES), 0) // DH
    lane = lax.broadcasted_iota(jnp.int32, (rows, LANES), 1) // DH
    return lane == (block if rows == DH else row)


def flip(place, r):
    for bit in (1 << i for i in range(r.bit_length()) if r >> i & 1):
        place = place + bit * (1 - 2 * ((place // bit) % 2))
    return place


def group_spans(groups):
    spans, start = [], 0
    for size in SPLIT:
        stop = min(groups, start + size)
        spans.append((start, stop))
        start = stop
    spans[-1] = (spans[-1][0], groups)
    return spans


def project(wbuf, rows, sublanes):
    return lax.dot_general(
        wbuf[sublanes, :], rows, (((1,), (1,)), ((), ())),
        preferred_element_type=jnp.float32,
    ).astype(jnp.bfloat16)


def attend_kernel(
    n, gsize, ff_ref, q_ref, k_ref, v_ref, w_ref, comb, wbuf, obuf,
    kbuf, vbuf, qbuf, own_att, frames, near_out, near_in, tot_out, a_in, b_out, b_in, c_out, c_in, fin, other,
    load_sem, late_sem, a_sem, b_sem, c_sem, near_sem, q_sem, fin_sem, comb_sem,
):
    fr, height = frames.shape[:2]
    ft = kbuf.shape[0] // fr
    groups = kbuf.shape[1] // LANES
    base = groups * DH
    part = height // gsize
    me = lax.axis_index("tm")
    core = lax.axis_index("cfg")
    other_core = 1 - core
    place, level = me % gsize, me // gsize
    levels = n // gsize
    share = other.shape[0]
    mine, theirs = core * share, other_core * share

    loads = []
    for f in range(fr):
        rows = pl.ds(f * ft, ft)
        for which, (src, dst) in enumerate(((k_ref, kbuf), (v_ref, vbuf))):
            copy = pltpu.make_async_copy(src.at[rows], dst.at[rows], load_sem.at[2 * f + which])
            copy.start()
            loads.append(copy)

    def mate(r):
        return {"tm": me - place + (flip(place, r))}

    barrier = pltpu.get_barrier_semaphore()
    pl.semaphore_signal(barrier, inc=1, device_id={"cfg": other_core})
    count = jnp.int32(gsize)
    for r in range(1, gsize):
        pl.semaphore_signal(barrier, inc=1, device_id=mate(r))
    for steps in [gsize * d for d in range(1, levels)] + list(range(1, NEAR + 1)):
        @pl.when(me >= steps)
        def _():
            pl.semaphore_signal(barrier, inc=1, device_id={"tm": me - steps})

        count = count + jnp.where(me + steps < n, 1, 0)

    masks = [head_mask(DH, a) for a in range(PER)]
    for f in range(fr):
        loads[2 * f].wait()
        loads[2 * f + 1].wait()
        frames[f, base:, :] = jnp.zeros((height - base, LANES), jnp.float32)
        for g in range(groups):
            cols = slice(g * LANES, (g + 1) * LANES)
            keys = jnp.maximum(kbuf[f * ft:(f + 1) * ft, cols], 0)
            values = vbuf[f * ft:(f + 1) * ft, cols]
            full = lax.dot_general(
                values, keys, (((0,), (0,)), ((), ())), preferred_element_type=jnp.float32
            )
            compact = jnp.zeros((DH, LANES), jnp.float32)
            for a in range(PER):
                compact = jnp.where(masks[a], full[a * DH:(a + 1) * DH], compact)
            frames[f, g * DH:(g + 1) * DH, :] = compact
            frames[f, base + g:base + g + 1, :] = jnp.sum(
                keys.astype(jnp.float32), axis=0, keepdims=True
            )
    columns = wbuf.shape[0]
    own_rows = pl.ds(pl.multiple_of(mine * ft, LANES), share * ft)
    their_rows = pl.ds(pl.multiple_of(theirs * ft, LANES), share * ft)
    late = [
        pltpu.make_async_copy(q_ref.at[own_rows], qbuf.at[0], late_sem.at[0]),
        pltpu.make_async_copy(
            w_ref.at[pl.ds(pl.multiple_of(core * columns, 16), columns)],
            wbuf, late_sem.at[1],
        ),
    ]
    for copy in late:
        copy.start()
    total = frames[0]
    for f in range(1, fr):
        total = total + frames[f]
    tot_out[...] = total.astype(jnp.bfloat16)
    near_out[...] = frames[...].astype(jnp.bfloat16)
    own_part = pl.ds(pl.multiple_of(place * part, 16), part)
    a_in[place] = tot_out[own_part, :]
    for d in range(1, NEAR + 1):
        @pl.when(me < d)
        def _():
            near_in[d - 1] = jnp.zeros(near_in.shape[1:], jnp.bfloat16)
    for d in range(1, levels):
        @pl.when(level < d)
        def _():
            b_in[d - 1] = jnp.zeros(b_in.shape[1:], jnp.bfloat16)

    pl.semaphore_wait(barrier, count)

    def a_copy(r):
        return pltpu.make_async_remote_copy(
            src_ref=tot_out.at[pl.ds(pl.multiple_of((flip(place, r)) * part, 16), part)],
            dst_ref=a_in.at[place], send_sem=a_sem.at[0, r - 1], recv_sem=a_sem.at[1, r - 1],
            device_id=mate(r),
        )

    def b_copy(d):
        return pltpu.make_async_remote_copy(
            src_ref=b_out, dst_ref=b_in.at[d - 1], send_sem=b_sem.at[0, d - 1],
            recv_sem=b_sem.at[1, d - 1], device_id={"tm": me + d * gsize},
        )

    def c_copy(r):
        return pltpu.make_async_remote_copy(
            src_ref=c_out.at[flip(place, r)], dst_ref=c_in.at[place], send_sem=c_sem.at[0, r - 1],
            recv_sem=c_sem.at[1, r - 1], device_id=mate(r),
        )

    def near_copy(d):
        return pltpu.make_async_remote_copy(
            src_ref=near_out, dst_ref=near_in.at[d - 1], send_sem=near_sem.at[0, d - 1],
            recv_sem=near_sem.at[1, d - 1], device_id={"tm": me + d},
        )

    q_copy = pltpu.make_async_remote_copy(
        src_ref=q_ref.at[their_rows], dst_ref=qbuf.at[1], send_sem=q_sem.at[0], recv_sem=q_sem.at[1],
        device_id={"cfg": other_core},
    )
    for r in reversed(range(1, gsize)):
        a_copy(r).start()
    for d in reversed(range(1, NEAR + 1)):
        @pl.when(me + d < n)
        def _():
            near_copy(d).start()
    q_copy.start()

    for r in range(1, gsize):
        a_copy(r).wait_recv()
    before = [jnp.zeros((part, LANES), jnp.float32)]
    for k in range(gsize):
        before.append(before[-1] + a_in[k].astype(jnp.float32))
    b_out[...] = before[-1].astype(jnp.bfloat16)
    for d in reversed(range(1, levels)):
        @pl.when(level + d < levels)
        def _():
            b_copy(d).start()
    for d in range(1, levels):
        @pl.when(level >= d)
        def _():
            b_copy(d).wait_recv()
    lower = jnp.zeros((part, LANES), jnp.float32)
    for d in range(1, levels):
        lower = lower + b_in[d - 1].astype(jnp.float32)
    for k in range(gsize):
        c_out[k] = (lower + before[k]).astype(jnp.bfloat16)
    for r in reversed(range(1, gsize)):
        c_copy(r).start()
    c_in[place] = c_out[place]
    for d in reversed(range(1, NEAR + 1)):
        @pl.when(me >= d)
        def _():
            near_copy(d).wait_recv()
    for r in range(1, gsize):
        c_copy(r).wait_recv()

    for j in range(fr):
        first = ff_ref[j]
        whole = first == 0
        acc = jnp.where(whole, 1.0, 0.0) * jnp.concatenate(
            [c_in[k].astype(jnp.float32) for k in range(gsize)], axis=0
        )
        for f in range(j + 1):
            acc = acc + jnp.where(me * fr + f >= first, 1.0, 0.0) * frames[f]
        for d in range(1, NEAR + 1):
            for f in range(fr):
                inside = jnp.logical_and(first > 0, (me - d) * fr + f >= first)
                acc = acc + jnp.where(inside, 1.0, 0.0) * near_in[d - 1, f].astype(jnp.float32)
        fin[j] = acc
    fin_copy = pltpu.make_async_remote_copy(
        src_ref=fin.at[pl.ds(theirs, share)], dst_ref=other, send_sem=fin_sem.at[0], recv_sem=fin_sem.at[1],
        device_id={"cfg": other_core},
    )
    fin_copy.start()

    own_scale = jnp.where(core == 0, guide_scale, 1.0 - guide_scale)
    other_scale = 1.0 - own_scale
    diagonal = head_mask(LANES, 0)

    def attended(b, source, f, i, g):
        compact = source[f, g * DH:(g + 1) * DH, :]
        sums = source[f, base + g:base + g + 1, :]
        state = jnp.where(diagonal, jnp.concatenate([compact] * PER, axis=0), 0.0)
        total = jnp.where(diagonal, jnp.broadcast_to(sums, (LANES, LANES)), 0.0)
        both = jnp.concatenate([state, total], axis=0)
        upper = both.astype(jnp.bfloat16)
        lower = (both - upper.astype(jnp.float32)).astype(jnp.bfloat16)
        feats = jnp.maximum(qbuf[b, i * ft:(i + 1) * ft, g * LANES:(g + 1) * LANES], 0)
        both = lax.dot_general(
            jnp.concatenate([feats, feats], axis=1),
            jnp.concatenate([upper, lower], axis=1),
            (((1,), (1,)), ((), ())), preferred_element_type=jnp.float32,
        )
        return both[:, :LANES] / (both[:, LANES:] + epsilon)

    late[0].wait()
    for i in range(share):
        for g in range(groups):
            own_att[i * ft:(i + 1) * ft, g * LANES:(g + 1) * LANES] = own_scale * attended(0, fin, mine + i, i, g)
    fin_copy.wait_recv()
    q_copy.wait_recv()
    comb_copies = []
    for s, (start, stop) in enumerate(group_spans(groups)):
        for g in range(start, stop):
            cols = slice(g * LANES, (g + 1) * LANES)
            for i in range(share):
                value = own_att[i * ft:(i + 1) * ft, cols] + other_scale * attended(1, other, i, i, g)
                comb[pl.ds(pl.multiple_of((mine + i) * ft, LANES), ft), cols] = value.astype(jnp.bfloat16)
        block = comb.at[own_rows, pl.ds(start * LANES, (stop - start) * LANES)]
        copy = pltpu.make_async_remote_copy(
            src_ref=block, dst_ref=block, send_sem=comb_sem.at[0, s], recv_sem=comb_sem.at[1, s],
            device_id={"cfg": other_core},
        )
        copy.start()
        comb_copies.append(copy)
    late[1].wait()
    rows = comb.shape[0]
    tile = pl.ds(pl.multiple_of(core * (rows - TILE), LANES), TILE)
    obuf[...] = project(wbuf, comb[tile, :], slice(0, columns))
    for copy in comb_copies:
        copy.wait()
    fin_copy.wait_send()
    q_copy.wait_send()
    for r in range(1, gsize):
        a_copy(r).wait_send()
        c_copy(r).wait_send()
    for d in range(1, levels):
        @pl.when(level + d < levels)
        def _():
            b_copy(d).wait_send()
    for d in range(1, NEAR + 1):
        @pl.when(me + d < n)
        def _():
            near_copy(d).wait_send()


def project_kernel(comb, wbuf, first, o_ref, obuf, sems):

    columns, rows = obuf.shape
    core = lax.axis_index("cfg")
    tile = TILE
    near = core * (rows - tile)
    far = (1 - core) * (rows - tile)
    span = pl.ds(pl.multiple_of(near, LANES), tile)
    copies = [pltpu.make_async_copy(first, o_ref.at[:, span], sems.at[0])]
    copies[0].start()
    starts = [tile * t for t in range(1, rows // tile - 1)] + [pl.multiple_of(far, LANES)]
    height = columns // PARTS
    for t, start in enumerate(starts):
        for h in range(PARTS):
            part = slice(h * height, (h + 1) * height)
            cols = pl.ds(start, tile)
            obuf[part, cols] = project(wbuf, comb[cols, :], part)
            copy = pltpu.make_async_copy(
                obuf.at[pl.ds(h * height, height), cols], o_ref.at[pl.ds(h * height, height), cols],
                sems.at[1 + t * PARTS + h],
            )
            copy.start()
            copies.append(copy)
    for copy in copies:
        copy.wait()


def on_device(n, cores, queries, key_vectors, value_vectors, out_weight, first_frame):
    rows, width = queries.shape[1:]
    fr = first_frame.shape[0]
    groups = width // LANES
    gsize = min(GROUP, n)
    levels = n // gsize
    height = groups * DH + groups
    height += -height % (16 * gsize)
    part = height // gsize
    share = fr // cores
    ft = rows // fr
    flat = lambda a: a.reshape(rows, width)
    f32, bf16 = jnp.float32, jnp.bfloat16
    hbm = pl.BlockSpec(memory_space=pltpu.HBM)
    vmem = pl.BlockSpec(memory_space=pltpu.VMEM)
    columns = out_weight.shape[1] // cores
    far = max(levels - 1, 1)
    dma = pltpu.SemaphoreType.DMA
    handed = 2 * (rows * width + columns * width + columns * TILE)
    comb, wbuf, obuf = pl.pallas_call(
        functools.partial(attend_kernel, n, gsize),
        name="attend",
        out_shape=[
            pltpu.VMEM((rows, width), bf16),
            pltpu.VMEM((columns, width), bf16),
            pltpu.VMEM((columns, TILE), bf16),
        ],
        in_specs=[pl.BlockSpec(memory_space=pltpu.SMEM), hbm, hbm, hbm, hbm],
        out_specs=[vmem] * 3,
        scratch_shapes=[
            pltpu.VMEM((rows, width), bf16),
            pltpu.VMEM((rows, width), bf16),
            pltpu.VMEM((2, share * ft, width), bf16),
            pltpu.VMEM((share * ft, width), f32),
            pltpu.VMEM((fr, height, LANES), f32),
            pltpu.VMEM((fr, height, LANES), bf16),
            pltpu.VMEM((NEAR, fr, height, LANES), bf16),
            pltpu.VMEM((height, LANES), bf16),
            pltpu.VMEM((gsize, part, LANES), bf16),
            pltpu.VMEM((part, LANES), bf16),
            pltpu.VMEM((far, part, LANES), bf16),
            pltpu.VMEM((gsize, part, LANES), bf16),
            pltpu.VMEM((gsize, part, LANES), bf16),
            pltpu.VMEM((fr, height, LANES), f32),
            pltpu.VMEM((share, height, LANES), f32),
            dma((2 * fr,)),
            dma((2,)),
            dma((2, gsize - 1)),
            dma((2, far)),
            dma((2, gsize - 1)),
            dma((2, NEAR)),
            dma((2,)),
            dma((2,)),
            dma((2, len(SPLIT))),
        ],
        compiler_params=pltpu.CompilerParams(
            collective_id=0, has_side_effects=True, vmem_limit_bytes=VMEM_BYTES - handed
        ),
    )(first_frame, flat(queries), flat(key_vectors), flat(value_vectors), out_weight.T)
    flipped = pl.pallas_call(
        project_kernel,
        name="project",
        out_shape=jax.ShapeDtypeStruct((columns, rows), bf16),
        in_specs=[vmem] * 3,
        out_specs=hbm,
        scratch_shapes=[
            pltpu.VMEM((columns, rows), bf16),
            dma((1 + PARTS * (rows // TILE),)),
        ],
        compiler_params=pltpu.CompilerParams(vmem_limit_bytes=40 * 2**20),
    )(comb, wbuf, obuf)
    return flipped.T


def solution(mesh):
    placed = (P("cfg", "tm", None), P("cfg", "tm", None), P("cfg", "tm", None), P(), P("tm"))
    return jax.shard_map(
        functools.partial(on_device, mesh.shape["tm"], mesh.shape["cfg"]),
        mesh=mesh, in_specs=placed, out_specs=P("tm", "cfg"), check_vma=False,
    )
```

time: 29.3 us -> 25.3 us (0.86)
  the two profiles are of different devices: /device:TPU:0 before, /device:TPU:9 now
where the time goes in v1:
time: 25.3 us; the launch traced here: 25.2 us
  Pallas kernels  25.2 us (100%)
    pallas_call x1, Pallas kernels, on_device(): pl.pallas_call(functools.partial(attend_kernel, n, gsize), name='attend',...  22.6 us
    pallas_call x1, Pallas kernels, on_device(): pl.pallas_call(project_kernel, name='project', out_shape=jax.ShapeDtypeSt...  2.57 us

profile of v1, /device:TPU:9, one launch (start us, length us, event | category | flops | bytes accessed | tf_op | source)
XLA Modules:
  0.0 25.2 jit_solution(3120544794037974836)
XLA Ops:
  0.0 22.6 %attend.1 = (bf16[768,1152]{1,0:T(8,128)(2,1)S(1)}, bf16[1120,1152]{1,0:T(8,128)(2,1)S(1)}, bf16[1120,256]{1,0:T(8,128)(2,1)S(1)}) custom-call(s32[2]{0:T(128)} %ff_ref.1, bf16[768,1152]{1,0:T(8,128)(2,1)} %bitcast.6, bf16[768,1152]{1,0:T(8,128)(2,1)} %bitcast.7, bf16[768,1152]{1,0:T(8,128)(2,1)} %bitcast.8, bf16[2240,1152]{1,0:T(8,128)(2,1)} %bitcast.5), custom_call_target="tpu_custom_call" | custom-call | tf_op jit(solution)/shard_map/attend/pallas_call | solution.py:335
  22.6 2.6 %project.1 = bf16[1120,768]{1,0:T(8,128)(2,1)} custom-call(bf16[768,1152]{1,0:T(8,128)(2,1)S(1)} %get-tuple-element.8.comb, bf16[1120,1152]{1,0:T(8,128)(2,1)S(1)} %get-tuple-element.9.wbuf, bf16[1120,256]{1,0:T(8,128)(2,1)S(1)} %get-tuple-element.10.first), custom_call_target="tpu_custom_call" | custom-call | tf_op jit(solution)/shard_map/project/pallas_call | solution.py:375
